TPU v7x, 256 devices: a whole 4x4x8 slice. The times are simulated.
256 devices in a mesh: section: 4 (over y), gy: 8 (over z), gx: 8 (over x, core).
Axes of the slice: x: 4, y: 4, z: 8, core: 2. Of those that a mesh axis runs over, the one named last changes fastest.
Arguments:
- level_input: bfloat16 [4, 4, 64, 128, 320], P('section', None, 'gy', 'gx'), may hold values from -72 to 72, as said below
- out_grad: bfloat16 [4, 4, 64, 128, 320], P('section', None, 'gy', 'gx'), may hold values from -6 to 6
- conv_weight: bfloat16 [4, 27, 320, 320], P('section'), may hold values from -0.0625 to 0.0625
- norm_gain: float32 [4, 320], P('section'), may hold values from 0.1 to 1.9
- norm_shift: float32 [4, 320], P('section'), may hold values from -3 to 3
Outputs:
- upstream_grad: bfloat16 [4, 4, 64, 128, 320], P('section', None, 'gy', 'gx')
- weight_grad: float32 [4, 8640, 320], P('section', ('gy', 'gx'))
- param_grad: float32 [4, 3, 320], P('section')
Inputs may be any that keep to these rules, and one draw needn't show every extreme that they name: `level_input`: level input values of order one with varying channel and position scales.
All inputs are finite; a program needn't handle non-finite values.
Results may differ from a plain program's by a relative error of at most 0.0029.
Values may be sent and summed in bfloat16 or wider, within the bound.
A program may use at most 128 MiB of HBM per device.

v0:
```python
import jax
import jax.numpy as jnp
from jax import lax
from jax.sharding import PartitionSpec as P

G = 32
eps = 1e-05


def from_everyone(shard, axis):
    count = lax.axis_size(axis)
    return lax.all_to_all(
        jnp.broadcast_to(shard[None], (count, *shard.shape)), axis, 0, 0, tiled=True
    )


def taken_together(shard, axis):
    everything = from_everyone(shard, axis)
    return jnp.sum(everything, axis=0)


def packed_total(arrays, axis):
    line, at, done = (jnp.concatenate([a.reshape(-1) for a in arrays]), 0, [])
    subtotal = taken_together(line, axis)
    for a in arrays:
        done.append(subtotal[at : at + a.size].reshape(a.shape))
        at += a.size
    return tuple(done)


def padded(block, sides, width):
    for axis, dim in sides:
        count = lax.axis_size(axis)
        forward = [(i, i + 1) for i in range(count - 1)]
        backward = [(target, source) for source, target in forward]
        low = lax.ppermute(
            lax.slice_in_dim(block, block.shape[dim] - width, None, axis=dim), axis, forward
        )
        high = lax.ppermute(lax.slice_in_dim(block, 0, width, axis=dim), axis, backward)
        block = jnp.concatenate([low, block, high], axis=dim)
    return block


def in_one(arrays, axis):
    ends = [0]
    for a in arrays:
        ends.append(ends[-1] + a.size)
    subtotal = lax.psum(jnp.concatenate([a.ravel() for a in arrays]), axis)
    return tuple((subtotal[b:e].reshape(a.shape) for a, b, e in zip(arrays, ends, ends[1:])))


def passed_along(shard, axis, by):
    count = lax.axis_size(axis)
    pairs = [(i, i + by) for i in range(count) if 0 <= i + by < count]
    return lax.ppermute(shard, axis, pairs)


def expand_groups(values, groups, per_group):
    return jnp.broadcast_to(values[:, None], (groups, per_group)).reshape(groups * per_group)


def local(level_input, out_grad, conv_weight, norm_gain, norm_shift):
    level_x = level_input[0]
    grad_cells = out_grad[0]
    kernel_all = conv_weight[0]
    gain_vec = norm_gain[0]
    shift_vec = norm_shift[0]
    frames, rows_h, cols_w, channels = level_x.shape
    groups = G
    per_group = channels // groups
    cell_count = frames * rows_h * cols_w
    members = cell_count * per_group * lax.axis_size("gy") * lax.axis_size("gx")
    x_float = level_x.astype(jnp.float32).reshape(cell_count, groups, per_group)
    sum_first, sum_second = packed_total(
        (jnp.sum(x_float, axis=(0, 2)), jnp.sum(x_float * x_float, axis=(0, 2))), ("gy", "gx")
    )
    group_mean = sum_first / members
    group_var = sum_second / members - group_mean * group_mean
    centered = x_float - group_mean[None, :, None]
    inv_std = 1.0 / jnp.sqrt(group_var + eps)
    normed = (centered * inv_std[None, :, None]).reshape(cell_count, channels)
    activ = normed * gain_vec[None, :] + shift_vec[None, :]
    sigmoid_v = jax.nn.sigmoid(activ)
    unit_rows = (activ * sigmoid_v).astype(jnp.bfloat16)
    extended = padded(grad_cells, (("gy", 1), ("gx", 2)), 1)
    framed = jnp.pad(extended, ((1, 1), (0, 0), (0, 0), (0, 0)))
    weight_pieces = []
    input_side = jnp.zeros((cell_count, channels), jnp.float32)
    for offset_f in range(3):
        for offset_h in range(3):
            for offset_w in range(3):
                kernel_idx = offset_f * 9 + offset_h * 3 + offset_w
                window = framed[
                    2 - offset_f : 2 - offset_f + frames,
                    2 - offset_h : 2 - offset_h + rows_h,
                    2 - offset_w : 2 - offset_w + cols_w,
                    :,
                ].reshape(cell_count, channels)
                input_side = input_side + lax.dot_general(
                    window,
                    kernel_all[kernel_idx],
                    (((1,), (1,)), ((), ())),
                    preferred_element_type=jnp.float32,
                )
                weight_pieces.append(
                    lax.dot_general(
                        unit_rows,
                        window,
                        (((0,), (0,)), ((), ())),
                        preferred_element_type=jnp.float32,
                    )
                )
    weight_part = lax.psum_scatter(
        jnp.concatenate(weight_pieces, axis=0), ("gy", "gx"), scatter_dimension=0, tiled=True
    )
    silu_slope = sigmoid_v * (1.0 + activ * (1.0 - sigmoid_v))
    act_grad = input_side * silu_slope
    grad_float = grad_cells.astype(jnp.float32).reshape(cell_count, channels)
    gain_sum, shift_sum, bias_sum = in_one(
        (
            jnp.sum(act_grad * normed, axis=0),
            jnp.sum(act_grad, axis=0),
            jnp.sum(grad_float, axis=0),
        ),
        ("gy", "gx"),
    )
    mean_first = jnp.sum((gain_vec * shift_sum).reshape(groups, per_group), axis=1) / members
    mean_second = jnp.sum((gain_vec * gain_sum).reshape(groups, per_group), axis=1) / members
    norm_grad = (
        act_grad * gain_vec[None, :]
        - expand_groups(mean_first, groups, per_group)[None, :]
        - normed * expand_groups(mean_second, groups, per_group)[None, :]
    ) * expand_groups(inv_std, groups, per_group)[None, :]
    level_grad = (
        (grad_float + norm_grad).astype(jnp.bfloat16).reshape(1, frames, rows_h, cols_w, channels)
    )
    upstream_grad = passed_along(level_grad, "section", -1)
    param_grad = jnp.stack([gain_sum, shift_sum, bias_sum])[None]
    return (upstream_grad, weight_part[None], param_grad)


def solution(mesh):
    return jax.shard_map(
        local,
        mesh=mesh,
        in_specs=(
            P("section", None, "gy", "gx", None),
            P("section", None, "gy", "gx", None),
            P("section", None, None, None),
            P("section", None),
            P("section", None),
        ),
        out_specs=(
            P("section", None, "gy", "gx", None),
            P("section", ("gy", "gx"), None),
            P("section", None, None),
        ),
        check_vma=False,
    )
```

profile of v0, /device:TPU:2, one launch (start us, length us, event | category | flops | bytes accessed | tf_op | source)
XLA Modules:
  0.0 333.8 jit_solution(14471769354519032061)
XLA Ops:
  7.2 1.2 convert_reduce_fusion.1
  9.5 12.0 %all-to-all-start = ((f32[64,1,64]{2,1,0:T(1,128)}), f32[64,1,64]{2,1,0:T(1,128)S(1)}, u32[]{:S(2)}, u32[]{:S(2)}) async-start(f32[64,1,64]{2,1,0:T(1,128)} %broadcast_in_dim.10), calls=%async_computation | async-start | bytes 65536 | tf_op jit(solution)/shard_map/all_to_all | solution.py:12
  22.5 1.3 collective-permute-start.1
  23.8 4.5 %collective-permute-start = (bf16[4,1,16,320]{3,2,1,0:T(8,128)(2,1)S(1)}, bf16[4,1,16,320]{3,2,1,0:T(8,128)(2,1)S(1)}, u32[]{:S(2)}, u32[]{:S(2)}) collective-permute-start(bf16[4,1,16,320]{3,2,1,0:T(8,128)(2,1)S(1)} %get-tuple-element.54), channel_id=1, source_target_pairs={{0,8},{8,16},{16,24},{24,32},{32,40},{40,48},{48,56},{1,9},{9,17},... | collective-permute-start | bytes 122888 | tf_op jit(solution)/shard_map/ppermute | solution.py:36
  28.3 1.7 convert_reduce_fusion
  30.0 2.0 copy.26
  33.4 1.9 copy.24
  35.9 1.3 multiply_convert_fusion
  37.2 2.2 convolution_bitcast_fusion
  39.4 1.2 pad_maximum_fusion.3
  40.6 1.9 collective-permute-start.3
  42.5 2.4 collective-permute-start.2
  45.0 1.2 pad_maximum_fusion.1
  46.2 1.2 fusion.83
  47.4 1.2 fusion.88
  49.1 1.9 fusion.68
  52.2 1.3 fusion.38
  54.2 2.5 fusion.26
  56.7 1.2 fusion.84
  57.9 1.2 fusion.74
  59.1 1.3 convolution_add_fusion.23
  61.5 1.3 convolution_add_fusion.22
  64.0 1.3 convolution_add_fusion.21
  65.3 1.2 fusion.77
  66.5 1.3 convolution_add_fusion.20
  69.0 1.3 convolution_add_fusion.19
  70.3 1.2 fusion.79
  71.5 1.3 convolution_add_fusion.18
  73.9 1.3 convolution_add_fusion.17
  75.2 1.2 fusion.81
  76.4 1.3 convolution_add_fusion.16
  78.9 2.2 convolution_add_fusion.15
  81.1 1.2 fusion.85
  82.3 1.2 fusion.86
  83.5 1.2 fusion.87
  84.7 1.2 fusion.89
  85.8 1.2 fusion.90
  87.1 1.2 fusion.91
  88.3 1.2 fusion.92
  91.8 1.2 fusion.95
  93.0 1.2 fusion.96
  95.3 1.2 fusion.98
  96.5 14.0 %concatenate.39 = f32[8640,320]{0,1:T(8,128)} concatenate(f32[320,320]{0,1:T(8,128)} %fusion.73, f32[320,320]{0,1:T(8,128)} %fusion.74, f32[320,320]{0,1:T(8,128)} %fusion.75, f32[320,320]{0,1:T(8,128)} %fusion.76, f32[320,320]{0,1:T(8,128)} %fusion.77, f32[320,320]{0,1:T(8,128)} %fusion.78, f32[320,320]{0,1:T(8,128)} %fusion.79, f32[320,320]{0,1:T(8,128)} %fusion.80, ...), dimensions={0} | concatenate | bytes 22118400 | tf_op jit(solution)/shard_map/concatenate | solution.py:114
  110.6 2.0 fusion.3
  112.6 1.4 fusion.19
  114.0 1.4 convolution_add_fusion.13
  115.4 1.3 convolution_add_fusion.12
  116.8 1.3 convolution_add_fusion.11
  118.1 1.3 convolution_add_fusion.10
  119.4 1.3 fusion.2
  120.7 1.3 convolution_add_fusion.8
  122.1 1.4 convolution_add_fusion.7
  123.5 1.3 convolution_add_fusion.6
  124.9 1.3 convolution_add_fusion.5
  126.2 1.4 convolution_add_fusion.4
  127.6 1.3 convolution_add_fusion.3
  129.0 1.3 convolution_add_fusion.2
  130.3 1.3 convolution_add_fusion.1
  131.7 1.6 multiply_reduce_fusion.1
  133.3 122.7 %psum.7 = f32[960]{0:T(1024)S(1)} all-reduce(f32[960]{0:T(1024)S(1)} %pad_maximum_fusion.7), channel_id=1, replica_groups=mesh['section'=4,'gy'=8,'gx'=8] {'gy','gx'}, use_global_device_ids=true, to_apply=%region_8.9 | all-reduce | flops 960 | bytes 7680 | tf_op jit(solution)/shard_map/psum | solution.py:48
  257.4 1.3 collective-permute-start.4
  260.6 6.5 %collective-permute-done.4 = bf16[1,4,8,16,320]{4,3,2,1,0:T(8,128)(2,1)S(1)} collective-permute-done((bf16[1,4,8,16,320]{4,3,2,1,0:T(8,128)(2,1)S(1)}, bf16[1,4,8,16,320]{4,3,2,1,0:T(8,128)(2,1)S(1)}, u32[]{:S(2)}, u32[]{:S(2)}) %collective-permute-start.4) | collective-permute-done | bytes 327712 | tf_op jit(solution)/shard_map/ppermute | solution.py:55
  267.1 57.1 %all-reduce.4.cloned.1.call-done = f32[8640,320]{0,1:T(8,128)} async-done(((f32[8640,320]{0,1:T(8,128)}), f32[8640,320]{0,1:T(8,128)}) %all-reduce.4.cloned.1.call-update) | async-done | bytes 11059216
  324.2 1.2 dynamic-slice_bitcast_fusion
  (114 shorter events, 19.9 us)
Async XLA Ops:
  7.2 41.5 %copy-start = (bf16[1,4,8,16,320]{4,3,2,1,0:T(8,128)(2,1)S(1)}, bf16[1,4,8,16,320]{4,3,2,1,0:T(8,128)(2,1)}, u32[]{:S(2)}) copy-start(bf16[1,4,8,16,320]{4,3,2,1,0:T(8,128)(2,1)} %param.6) | copy-start | bytes 983044
  9.5 25.8 %all-to-all-start = ((f32[64,1,64]{2,1,0:T(1,128)}), f32[64,1,64]{2,1,0:T(1,128)S(1)}, u32[]{:S(2)}, u32[]{:S(2)}) async-start(f32[64,1,64]{2,1,0:T(1,128)} %broadcast_in_dim.10), calls=%async_computation | async-start | bytes 65536 | tf_op jit(solution)/shard_map/all_to_all | solution.py:12
  21.6 302.6 %all-reduce.4.cloned.1.call-start = ((), (), s32[]{:S(2)}) async-start(), calls=%async_computation.1 | async-start | bytes 22282240
  22.5 16.9 %collective-permute-start.1 = (bf16[4,1,16,320]{3,2,1,0:T(8,128)(2,1)S(1)}, bf16[4,1,16,320]{3,2,1,0:T(8,128)(2,1)S(1)}, u32[]{:S(2)}, u32[]{:S(2)}) collective-permute-start(bf16[4,1,16,320]{3,2,1,0:T(8,128)(2,1)S(1)} %get-tuple-element.55), channel_id=1, source_target_pairs={{8,0},{16,8},{24,16},{32,24},{40,32},{48,40},{56,48},{9,1},{17,9},... | collective-permute-start | bytes 122888 | tf_op jit(solution)/shard_map/ppermute | solution.py:39
  23.8 15.6 %collective-permute-start = (bf16[4,1,16,320]{3,2,1,0:T(8,128)(2,1)S(1)}, bf16[4,1,16,320]{3,2,1,0:T(8,128)(2,1)S(1)}, u32[]{:S(2)}, u32[]{:S(2)}) collective-permute-start(bf16[4,1,16,320]{3,2,1,0:T(8,128)(2,1)S(1)} %get-tuple-element.54), channel_id=1, source_target_pairs={{0,8},{8,16},{16,24},{24,32},{32,40},{40,48},{48,56},{1,9},{9,17},... | collective-permute-start | bytes 122888 | tf_op jit(solution)/shard_map/ppermute | solution.py:36
  32.7 9.8 %copy-start.26 = (f32[320]{0:T(512)}, f32[320]{0:T(512)S(1)}, u32[]{:S(2)}) copy-start(f32[320]{0:T(512)S(1)} %reduce.7) | copy-start | bytes 3844
  33.4 9.1 %copy-start.19 = (f32[320]{0:T(512)}, f32[320]{0:T(512)S(1)}, u32[]{:S(2)}) copy-start(f32[320]{0:T(512)S(1)} %reduce.6) | copy-start | bytes 3844
  35.7 6.8 %copy-start.21 = (f32[320]{0:T(512)}, f32[320]{0:T(512)S(1)}, u32[]{:S(2)}) copy-start(f32[320]{0:T(512)S(1)} %mul.173) | copy-start | bytes 3844
  35.9 6.7 %copy-start.23 = (f32[320]{0:T(512)}, f32[320]{0:T(512)S(1)}, u32[]{:S(2)}) copy-start(f32[320]{0:T(512)S(1)} %sub.64) | copy-start | bytes 3844
  39.4 9.2 %copy-start.15 = (bf16[4,1,16,320]{3,2,1,0:T(8,128)(2,1)}, bf16[4,1,16,320]{3,2,1,0:T(8,128)(2,1)S(1)}, u32[]{:S(2)}) copy-start(bf16[4,1,16,320]{3,2,1,0:T(8,128)(2,1)S(1)} %collective-permute-done.1) | copy-start | bytes 122884
  39.4 9.2 %copy-start.17 = (bf16[4,1,16,320]{3,2,1,0:T(8,128)(2,1)}, bf16[4,1,16,320]{3,2,1,0:T(8,128)(2,1)S(1)}, u32[]{:S(2)}) copy-start(bf16[4,1,16,320]{3,2,1,0:T(8,128)(2,1)S(1)} %collective-permute-done) | copy-start | bytes 122884
  40.6 8.0 %collective-permute-start.3 = (bf16[4,10,1,320]{3,2,1,0:T(2,128)(2,1)S(1)}, bf16[4,10,1,320]{3,2,1,0:T(2,128)(2,1)S(1)}, u32[]{:S(2)}, u32[]{:S(2)}) collective-permute-start(bf16[4,10,1,320]{3,2,1,0:T(2,128)(2,1)S(1)} %get-tuple-element.50), channel_id=1, source_target_pairs={{1,0},{2,1},{3,2},{4,3},{5,4},{6,5},{7,6},{9,8},{10,9},{11,10},{12... | collective-permute-start | bytes 76808 | tf_op jit(solution)/shard_map/ppermute | solution.py:39
  42.5 6.0 %collective-permute-start.2 = (bf16[4,10,1,320]{3,2,1,0:T(2,128)(2,1)S(1)}, bf16[4,10,1,320]{3,2,1,0:T(2,128)(2,1)S(1)}, u32[]{:S(2)}, u32[]{:S(2)}) collective-permute-start(bf16[4,10,1,320]{3,2,1,0:T(2,128)(2,1)S(1)} %get-tuple-element.51), channel_id=1, source_target_pairs={{0,1},{1,2},{2,3},{3,4},{4,5},{5,6},{6,7},{8,9},{9,10},{10,11},{11... | collective-permute-start | bytes 76808 | tf_op jit(solution)/shard_map/ppermute | solution.py:36
  46.2 2.4 copy-start.1
  46.2 2.4 copy-start.3
  49.1 4.4 %copy-start.16 = (bf16[4,1,16,320]{3,2,1,0:T(8,128)(2,1)S(1)}, bf16[4,1,16,320]{3,2,1,0:T(8,128)(2,1)}, u32[]{:S(2)}) copy-start(bf16[4,1,16,320]{3,2,1,0:T(8,128)(2,1)} %copy-done.15) | copy-start | bytes 122884
  49.1 4.4 %copy-start.18 = (bf16[4,1,16,320]{3,2,1,0:T(8,128)(2,1)S(1)}, bf16[4,1,16,320]{3,2,1,0:T(8,128)(2,1)}, u32[]{:S(2)}) copy-start(bf16[4,1,16,320]{3,2,1,0:T(8,128)(2,1)} %copy-done.17) | copy-start | bytes 122884
  51.0 44.3 %copy-start.12 = (bf16[4,8,16,320]{3,2,1,0:T(8,128)(2,1)}, bf16[4,8,16,320]{3,2,1,0:T(8,128)(2,1)S(1)}, u32[]{:S(2)}) copy-start(bf16[4,8,16,320]{3,2,1,0:T(8,128)(2,1)S(1)} %get-tuple-element.24) | copy-start | bytes 983044
  54.2 26.9 %copy-start.9 = (bf16[4,8,16,320]{3,2,1,0:T(8,128)(2,1)}, bf16[4,8,16,320]{3,2,1,0:T(8,128)(2,1)S(1)}, u32[]{:S(2)}) copy-start(bf16[4,8,16,320]{3,2,1,0:T(8,128)(2,1)S(1)} %get-tuple-element.43) | copy-start | bytes 983044
  54.2 28.1 %copy-start.7 = (bf16[4,8,16,320]{3,2,1,0:T(8,128)(2,1)}, bf16[4,8,16,320]{3,2,1,0:T(8,128)(2,1)S(1)}, u32[]{:S(2)}) copy-start(bf16[4,8,16,320]{3,2,1,0:T(8,128)(2,1)S(1)} %get-tuple-element.64) | copy-start | bytes 983044
  54.2 29.3 %copy-start.5 = (bf16[4,8,16,320]{3,2,1,0:T(8,128)(2,1)}, bf16[4,8,16,320]{3,2,1,0:T(8,128)(2,1)S(1)}, u32[]{:S(2)}) copy-start(bf16[4,8,16,320]{3,2,1,0:T(8,128)(2,1)S(1)} %get-tuple-element.42) | copy-start | bytes 983044
  54.2 30.4 %copy-start.4 = (bf16[4,8,16,320]{3,2,1,0:T(8,128)(2,1)}, bf16[4,8,16,320]{3,2,1,0:T(8,128)(2,1)S(1)}, u32[]{:S(2)}) copy-start(bf16[4,8,16,320]{3,2,1,0:T(8,128)(2,1)S(1)} %get-tuple-element.63) | copy-start | bytes 983044
  110.6 6.2 %copy-start.8 = (bf16[4,8,16,320]{3,2,1,0:T(8,128)(2,1)S(1)}, bf16[4,8,16,320]{3,2,1,0:T(8,128)(2,1)}, u32[]{:S(2)}) copy-start(bf16[4,8,16,320]{3,2,1,0:T(8,128)(2,1)} %copy-done.7) | copy-start | bytes 983044
  110.6 7.5 %copy-start.6 = (bf16[4,8,16,320]{3,2,1,0:T(8,128)(2,1)S(1)}, bf16[4,8,16,320]{3,2,1,0:T(8,128)(2,1)}, u32[]{:S(2)}) copy-start(bf16[4,8,16,320]{3,2,1,0:T(8,128)(2,1)} %copy-done.5) | copy-start | bytes 983044
  110.6 8.8 %copy-start.2 = (bf16[4,8,16,320]{3,2,1,0:T(8,128)(2,1)S(1)}, bf16[4,8,16,320]{3,2,1,0:T(8,128)(2,1)}, u32[]{:S(2)}) copy-start(bf16[4,8,16,320]{3,2,1,0:T(8,128)(2,1)} %copy-done.1) | copy-start | bytes 983044
  122.1 9.6 %copy-start.10 = (f32[512,320]{0,1:T(8,128)S(1)}, f32[512,320]{0,1:T(8,128)}, u32[]{:S(2)}) copy-start(f32[512,320]{0,1:T(8,128)} %copy.26) | copy-start | bytes 1966084
  122.1 9.6 %copy-start.13 = (bf16[4,8,16,320]{3,2,1,0:T(8,128)(2,1)S(1)}, bf16[4,8,16,320]{3,2,1,0:T(8,128)(2,1)}, u32[]{:S(2)}) copy-start(bf16[4,8,16,320]{3,2,1,0:T(8,128)(2,1)} %copy-done.12) | copy-start | bytes 983044
  122.1 9.6 %copy-start.20 = (f32[320]{0:T(512)S(1)}, f32[320]{0:T(512)}, u32[]{:S(2)}) copy-start(f32[320]{0:T(512)} %copy-done.19) | copy-start | bytes 3844
  122.1 9.6 %copy-start.22 = (f32[320]{0:T(512)S(1)}, f32[320]{0:T(512)}, u32[]{:S(2)}) copy-start(f32[320]{0:T(512)} %copy-done.21) | copy-start | bytes 3844
  122.1 9.6 %copy-start.24 = (f32[320]{0:T(512)S(1)}, f32[320]{0:T(512)}, u32[]{:S(2)}) copy-start(f32[320]{0:T(512)} %copy-done.23) | copy-start | bytes 3844
  122.1 9.6 %copy-start.27 = (f32[320]{0:T(512)S(1)}, f32[320]{0:T(512)}, u32[]{:S(2)}) copy-start(f32[320]{0:T(512)} %copy-done.26) | copy-start | bytes 3844
  126.2 7.1 %copy-start.25 = (f32[320]{0:T(512)S(1)}, f32[320]{0:T(512)}, u32[]{:S(2)}) copy-start(f32[320]{0:T(512)} %convert_reduce_fusion) | copy-start | bytes 3844
  126.2 130.6 %copy-start.11 = (f32[512,320]{0,1:T(8,128)S(1)}, f32[512,320]{0,1:T(8,128)}, u32[]{:S(2)}) copy-start(f32[512,320]{0,1:T(8,128)} %copy.26) | copy-start | bytes 1966084
  126.2 130.6 %copy-start.14 = (bf16[512,320]{0,1:T(8,128)(2,1)S(1)}, bf16[512,320]{0,1:T(8,128)(2,1)}, u32[]{:S(2)}) copy-start(bf16[512,320]{0,1:T(8,128)(2,1)} %copy.24) | copy-start | bytes 983044
  128.9 129.7 %copy-start.28 = (u32[256]{0:T(256)S(1)}, u32[256]{0:T(256)}, u32[]{:S(2)}) copy-start(u32[256]{0:T(256)} %constant.25) | copy-start | bytes 3076
  257.4 9.7 %collective-permute-start.4 = (bf16[1,4,8,16,320]{4,3,2,1,0:T(8,128)(2,1)S(1)}, bf16[1,4,8,16,320]{4,3,2,1,0:T(8,128)(2,1)S(1)}, u32[]{:S(2)}, u32[]{:S(2)}) collective-permute-start(bf16[1,4,8,16,320]{4,3,2,1,0:T(8,128)(2,1)S(1)} %bitcast.295), channel_id=1, source_target_pairs={{64,0},{128,64},{192,128},{65,1},{129,65},{193,129},{66,2},{130,66... | collective-permute-start | bytes 983048 | tf_op jit(solution)/shard_map/ppermute | solution.py:55
Sparse Core Ops, SparseCore 0:
  110.7 213.4 all-reduce.3
where the time goes:
time: 337 us; the launch traced here: 334 us
  blocking collectives  123 us (36%)
  matrix products  71.6 us (21%)
  waiting for transfers between devices  63.6 us (19%)
  local copies, waits for them, and re-layouts  27.1 us (8%)
  starting transfers between devices  23.5 us (7%)
  between operations  15.5 us (5%)
  other arithmetic  9.78 us (3%)
    psum x1, blocking collectives, in_one(): subtotal = lax.psum(jnp.concatenate([a.ravel() for a in arrays]), axis)  123 us
    unnamed x2, waiting for transfers between devices  57.1 us
    dot_general x27, matrix products, local(): lax.dot_general(window, kernel_all[kernel_idx], (((1,), (1,)), ((), ())),...  38.7 us
    dot_general x27, matrix products, local(): lax.dot_general(unit_rows, window, (((0,), (0,)), ((), ())), preferred_el...  32.9 us
    concatenate x1, local copies, waits for them, and re-layouts, local(): jnp.concatenate(weight_pieces, axis=0)  14 us
    all_to_all x1, starting transfers between devices, from_everyone(): lax.all_to_all(jnp.broadcast_to(shard[None], (count, *shard.shape)), axis...  12 us
    ppermute x2, starting transfers between devices, padded(): lax.ppermute(lax.slice_in_dim(block, block.shape[dim] - width, None, axis...  6.95 us
  transfers between devices with their start and end apart: 7, of which 2 were waited for; matrix products, arithmetic and copies ran while one was open for 12% of the time, Pallas kernels for 0%

commit v1 on v0

--- a/solution.py
+++ b/solution.py
@@ -45,7 +45,7 @@
     ends = [0]
     for a in arrays:
         ends.append(ends[-1] + a.size)
-    subtotal = lax.psum(jnp.concatenate([a.ravel() for a in arrays]), axis)
+    subtotal = jnp.sum(lax.all_gather(jnp.concatenate([a.ravel() for a in arrays]), axis), axis=0)
     return tuple((subtotal[b:e].reshape(a.shape) for a, b, e in zip(arrays, ends, ends[1:])))
 
 

time: 337 us -> 366 us (1.086)
  waiting for transfers between devices: 63.6 us -> 220 us
  blocking collectives: 123 us -> 0 us
  matrix products: 71.6 us -> 65.6 us
    unnamed x2, waiting for transfers between devices: 57.1 us -> 213 us
    psum x1 -> x0, blocking collectives: 123 us -> none  [in_one(): subtotal = lax.psum(jnp.concatenate([a.ravel() for a in arrays]), axis)]
    dot_general x27, matrix products: 32.9 us -> 29 us  [local(): lax.dot_general(unit_rows, window, (((0,), (0,)), ((), ())), preferred_el...]
  transfers between devices with their start and end apart: 7 -> 7, of which waited for: 2 -> 3; matrix products, arithmetic and copies ran while one was open for 12% -> 4% of each run, Pallas kernels for 0% -> 0%
where the time goes in v1:
time: 366 us; the launch traced here: 363 us
  waiting for transfers between devices  220 us (60%)
  matrix products  65.6 us (18%)
  local copies, waits for them, and re-layouts  26.9 us (7%)
  starting transfers between devices  23.5 us (6%)
  between operations  15.9 us (4%)
  other arithmetic  10.6 us (3%)
    unnamed x2, waiting for transfers between devices  213 us
    dot_general x27, matrix products, local(): lax.dot_general(window, kernel_all[kernel_idx], (((1,), (1,)), ((), ())),...  36.5 us
    dot_general x27, matrix products, local(): lax.dot_general(unit_rows, window, (((0,), (0,)), ((), ())), preferred_el...  29 us
    concatenate x1, local copies, waits for them, and re-layouts, local(): jnp.concatenate(weight_pieces, axis=0)  14 us
    all_to_all x1, starting transfers between devices, from_everyone(): lax.all_to_all(jnp.broadcast_to(shard[None], (count, *shard.shape)), axis...  12 us
  transfers between devices with their start and end apart: 7, of which 3 were waited for; matrix products, arithmetic and copies ran while one was open for 4% of the time, Pallas kernels for 0%

profile of v1, /device:TPU:2, one launch (start us, length us, event | category | flops | bytes accessed | tf_op | source)
XLA Modules:
  0.0 362.8 jit_solution(13786232980169760455)
XLA Ops:
  7.2 1.2 convert_reduce_fusion.1
  9.5 12.0 %all-to-all-start = ((f32[64,1,64]{2,1,0:T(1,128)}), f32[64,1,64]{2,1,0:T(1,128)S(1)}, u32[]{:S(2)}, u32[]{:S(2)}) async-start(f32[64,1,64]{2,1,0:T(1,128)} %broadcast_in_dim.10), calls=%async_computation | async-start | bytes 65536 | tf_op jit(solution)/shard_map/all_to_all | solution.py:12
  22.5 1.3 collective-permute-start.1
  23.8 4.5 %collective-permute-start = (bf16[4,1,16,320]{3,2,1,0:T(8,128)(2,1)S(1)}, bf16[4,1,16,320]{3,2,1,0:T(8,128)(2,1)S(1)}, u32[]{:S(2)}, u32[]{:S(2)}) collective-permute-start(bf16[4,1,16,320]{3,2,1,0:T(8,128)(2,1)S(1)} %get-tuple-element.56), channel_id=1, source_target_pairs={{0,8},{8,16},{16,24},{24,32},{32,40},{40,48},{48,56},{1,9},{9,17},... | collective-permute-start | bytes 122888 | tf_op jit(solution)/shard_map/ppermute | solution.py:36
  32.0 1.3 fusion.73
  34.5 1.3 multiply_convert_fusion
  35.8 1.4 convolution_bitcast_fusion
  38.3 1.9 collective-permute-start.3
  40.2 2.4 collective-permute-start.2
  42.6 1.2 pad_maximum_fusion.1
  46.2 1.9 fusion.68
  48.5 1.3 fusion.38
  50.5 1.3 fusion.26
  52.2 1.3 fusion.19
  53.5 1.2 fusion.90
  54.7 1.2 fusion.75
  55.9 1.3 convolution_add_fusion.23
  57.2 1.2 fusion.76
  58.4 1.3 convolution_add_fusion.22
  59.7 1.2 fusion.77
  60.9 1.3 convolution_add_fusion.21
  62.2 1.2 fusion.78
  63.4 1.3 convolution_add_fusion.20
  64.7 1.2 fusion.79
  65.9 1.3 convolution_add_fusion.19
  67.2 1.2 fusion.80
  68.4 1.3 convolution_add_fusion.18
  69.8 1.2 fusion.81
  70.9 1.3 convolution_add_fusion.17
  72.2 1.2 fusion.82
  73.5 1.3 convolution_add_fusion.16
  74.8 1.2 fusion.83
  76.0 1.3 convolution_add_fusion.15
  77.3 1.2 fusion.86
  78.5 1.3 fusion.3
  79.8 1.3 convolution_add_fusion.13
  81.1 1.2 fusion.87
  82.3 1.3 convolution_add_fusion.12
  83.6 1.3 convolution_add_fusion.11
  84.9 1.2 fusion.88
  86.1 1.3 convolution_add_fusion.10
  88.6 1.3 fusion.2
  90.0 1.3 convolution_add_fusion.8
  91.3 1.2 fusion.92
  92.5 1.3 convolution_add_fusion.7
  93.8 1.2 fusion.93
  95.0 1.3 convolution_add_fusion.6
  96.3 1.2 fusion.94
  97.4 1.3 convolution_add_fusion.5
  98.8 1.2 fusion.95
  100.0 1.3 convolution_add_fusion.4
  102.5 1.3 convolution_add_fusion.3
  103.8 1.2 fusion.97
  105.0 1.5 convolution_add_fusion.2
  106.5 1.2 fusion.98
  107.7 1.3 convolution_add_fusion.1
  109.0 1.2 fusion.99
  110.2 2.3 multiply_reduce_fusion.1
  113.2 1.4 maximum_dynamic-update-slice_fusion
  114.6 14.0 %concatenate.39 = f32[8640,320]{0,1:T(8,128)} concatenate(f32[320,320]{0,1:T(8,128)S(1)} %fusion.74, f32[320,320]{0,1:T(8,128)} %fusion.75, f32[320,320]{0,1:T(8,128)} %fusion.76, f32[320,320]{0,1:T(8,128)} %fusion.77, f32[320,320]{0,1:T(8,128)} %fusion.78, f32[320,320]{0,1:T(8,128)} %fusion.79, f32[320,320]{0,1:T(8,128)} %fusion.80, f32[320,320]{0,1:T(8,128)} %fusion.81, ...), dimensions={0} | concatenate | bytes 22118400 | tf_op jit(solution)/shard_map/concatenate | solution.py:114
  128.9 213.1 %all-reduce.6.cloned.1.call-done = (f32[61440]{0:T(1024)}, f32[8640,320]{0,1:T(8,128)}) async-done(((f32[61440]{0:T(1024)}, f32[8640,320]{0,1:T(8,128)}), (f32[61440]{0:T(1024)}, f32[8640,320]{0,1:T(8,128)})) %all-reduce.6.cloned.1.call-update) | async-done | bytes 11304976
  344.4 1.3 collective-permute-start.4
  346.4 1.2 dynamic-slice_bitcast_fusion
  349.0 6.2 %collective-permute-done.4 = bf16[1,4,8,16,320]{4,3,2,1,0:T(8,128)(2,1)S(1)} collective-permute-done((bf16[1,4,8,16,320]{4,3,2,1,0:T(8,128)(2,1)S(1)}, bf16[1,4,8,16,320]{4,3,2,1,0:T(8,128)(2,1)S(1)}, u32[]{:S(2)}, u32[]{:S(2)}) %collective-permute-start.4) | collective-permute-done | bytes 327712 | tf_op jit(solution)/shard_map/ppermute | solution.py:55
  (62 shorter events, 18.9 us)
Async XLA Ops:
  7.2 38.6 %copy-start = (bf16[1,4,8,16,320]{4,3,2,1,0:T(8,128)(2,1)S(1)}, bf16[1,4,8,16,320]{4,3,2,1,0:T(8,128)(2,1)}, u32[]{:S(2)}) copy-start(bf16[1,4,8,16,320]{4,3,2,1,0:T(8,128)(2,1)} %param.6) | copy-start | bytes 983044
  9.5 24.4 %all-to-all-start = ((f32[64,1,64]{2,1,0:T(1,128)}), f32[64,1,64]{2,1,0:T(1,128)S(1)}, u32[]{:S(2)}, u32[]{:S(2)}) async-start(f32[64,1,64]{2,1,0:T(1,128)} %broadcast_in_dim.10), calls=%async_computation | async-start | bytes 65536 | tf_op jit(solution)/shard_map/all_to_all | solution.py:12
  21.6 320.4 %all-reduce.6.cloned.1.call-start = ((), (), s32[]{:S(2)}) async-start(), calls=%async_computation.1 | async-start | bytes 22773760
  22.5 14.7 %collective-permute-start.1 = (bf16[4,1,16,320]{3,2,1,0:T(8,128)(2,1)S(1)}, bf16[4,1,16,320]{3,2,1,0:T(8,128)(2,1)S(1)}, u32[]{:S(2)}, u32[]{:S(2)}) collective-permute-start(bf16[4,1,16,320]{3,2,1,0:T(8,128)(2,1)S(1)} %get-tuple-element.57), channel_id=1, source_target_pairs={{8,0},{16,8},{24,16},{32,24},{40,32},{48,40},{56,48},{9,1},{17,9},... | collective-permute-start | bytes 122888 | tf_op jit(solution)/shard_map/ppermute | solution.py:39
  23.8 13.4 %collective-permute-start = (bf16[4,1,16,320]{3,2,1,0:T(8,128)(2,1)S(1)}, bf16[4,1,16,320]{3,2,1,0:T(8,128)(2,1)S(1)}, u32[]{:S(2)}, u32[]{:S(2)}) collective-permute-start(bf16[4,1,16,320]{3,2,1,0:T(8,128)(2,1)S(1)} %get-tuple-element.56), channel_id=1, source_target_pairs={{0,8},{8,16},{16,24},{24,32},{32,40},{40,48},{48,56},{1,9},{9,17},... | collective-permute-start | bytes 122888 | tf_op jit(solution)/shard_map/ppermute | solution.py:36
  38.3 6.4 %collective-permute-start.3 = (bf16[4,10,1,320]{3,2,1,0:T(2,128)(2,1)S(1)}, bf16[4,10,1,320]{3,2,1,0:T(2,128)(2,1)S(1)}, u32[]{:S(2)}, u32[]{:S(2)}) collective-permute-start(bf16[4,10,1,320]{3,2,1,0:T(2,128)(2,1)S(1)} %get-tuple-element.52), channel_id=1, source_target_pairs={{1,0},{2,1},{3,2},{4,3},{5,4},{6,5},{7,6},{9,8},{10,9},{11,10},{12... | collective-permute-start | bytes 76808 | tf_op jit(solution)/shard_map/ppermute | solution.py:39
  40.2 5.5 %collective-permute-start.2 = (bf16[4,10,1,320]{3,2,1,0:T(2,128)(2,1)S(1)}, bf16[4,10,1,320]{3,2,1,0:T(2,128)(2,1)S(1)}, u32[]{:S(2)}, u32[]{:S(2)}) collective-permute-start(bf16[4,10,1,320]{3,2,1,0:T(2,128)(2,1)S(1)} %get-tuple-element.53), channel_id=1, source_target_pairs={{0,1},{1,2},{2,3},{3,4},{4,5},{5,6},{6,7},{8,9},{9,10},{10,11},{11... | collective-permute-start | bytes 76808 | tf_op jit(solution)/shard_map/ppermute | solution.py:36
  128.6 215.3 %copy-start.1 = (f32[512,320]{0,1:T(8,128)S(1)}, f32[512,320]{0,1:T(8,128)}, u32[]{:S(2)}) copy-start(f32[512,320]{0,1:T(8,128)} %get-tuple-element.65) | copy-start | bytes 1966084
  344.4 10.8 %collective-permute-start.4 = (bf16[1,4,8,16,320]{4,3,2,1,0:T(8,128)(2,1)S(1)}, bf16[1,4,8,16,320]{4,3,2,1,0:T(8,128)(2,1)S(1)}, u32[]{:S(2)}, u32[]{:S(2)}) collective-permute-start(bf16[1,4,8,16,320]{4,3,2,1,0:T(8,128)(2,1)S(1)} %bitcast.296), channel_id=1, source_target_pairs={{64,0},{128,64},{192,128},{65,1},{129,65},{193,129},{66,2},{130,66... | collective-permute-start | bytes 983048 | tf_op jit(solution)/shard_map/ppermute | solution.py:55
Sparse Core Ops, SparseCore 0:
  128.8 213.1 all-reduce.5
